TPU v7x, 128 devices: a whole 4x4x4 slice. The times are simulated.
128 devices in a mesh: dp: 8 (over y, x_lo), tp: 16 (over z, x_hi, core).
Axes of the slice: x: 4 (x_hi: 2, x_lo: 2; x = x_hi * 2 + x_lo), y: 4, z: 4, core: 2. Of those that a mesh axis runs over, the one named last changes fastest.
Arguments:
- gradients: bfloat16 [8, 4, 3072, 768], P('dp', None, 'tp'), may hold values from -6 to 6, as said below
- right_factor: float32 [4, 768, 8], replicated, may hold values from -6 to 6
- weights_before: float32 [4, 3072, 768], P(None, 'tp', 'dp'), may hold values from -0.21875 to 0.21875
- momentum: float32 [4, 3072, 768], P(None, 'tp', 'dp'), may hold values from -0.3125 to 0.3125
Outputs:
- new_weights: float32 [4, 3072, 768], P(None, 'tp', 'dp')
- new_basis: float32 [4, 768, 8], replicated
- new_momentum: float32 [4, 3072, 768], P(None, 'tp', 'dp')
Inputs may be any that keep to these rules, and one draw needn't show every extreme that they name: gradients holds numbers from -6 to 6.
All inputs are finite; a program needn't handle non-finite values.
Results may differ from a plain program's by a relative error of at most 0.0003.
Values sent between devices are 32-bit elements.
A program may use at most 64 MiB of HBM per device.

v0:
```python
import jax
import jax.numpy as jnp
from jax import lax
from jax.sharding import Mesh
from jax.sharding import PartitionSpec as P

RANK = 8
DP = ("dp_0", "dp_1")
DP_TP = ("dp_0", "dp_1", "tp")


def by_axis(x, axes):
    for axis in axes:
        x = lax.psum(x, axis)
    return x


def on_device(gradients, right_factor, weights_before, momentum):
    own_grads = gradients[0]
    part_left = jnp.einsum(
        "liw,lwr->lir",
        own_grads,
        right_factor.astype(jnp.bfloat16),
        preferred_element_type=jnp.float32,
    )
    left = by_axis(part_left, DP)
    part_gram = jnp.einsum("lir,lis->lrs", left, left, precision=lax.Precision.HIGHEST)
    small_left = left.astype(jnp.bfloat16)
    part_right = jnp.einsum(
        "liw,lir->lwr", own_grads, small_left, preferred_element_type=jnp.float32
    )
    own_share = part_gram / lax.axis_size(DP)
    right, gram = lax.psum((part_right, own_share), DP_TP)
    gram = gram + 0.001 * jnp.mean(jnp.diagonal(gram, axis1=1, axis2=2), axis=1)[
        :, None, None
    ] * jnp.eye(RANK, dtype=jnp.float32)
    place = lax.axis_index(DP) * weights_before.shape[2]
    own_right = lax.dynamic_slice_in_dim(right, place, weights_before.shape[2], axis=1)
    root = jnp.linalg.cholesky(gram)
    half = lax.linalg.triangular_solve(
        root, jnp.swapaxes(own_right, 1, 2), left_side=True, lower=True
    )
    mixed = lax.linalg.triangular_solve(root, half, left_side=True, lower=True, transpose_a=True)
    change = jnp.einsum(
        "lir,lrw->liw", left, mixed, precision=lax.Precision.HIGHEST
    ) / lax.axis_size(DP)
    new_momentum = 0.9 * momentum + change
    new_weights = weights_before - 0.02 * new_momentum
    new_basis = right * lax.rsqrt(jnp.mean(right * right, axis=(1, 2), keepdims=True) + 1e-12)
    return (new_weights, new_basis, new_momentum)


def solution(mesh):
    split = Mesh(mesh.devices.reshape(4, 2, mesh.shape["tp"]), ("dp_0", "dp_1", "tp"))
    in_specs = (P(DP, None, "tp", None), P(), P(None, "tp", DP), P(None, "tp", DP))
    out_specs = (P(None, "tp", DP), P(), P(None, "tp", DP))
    return jax.shard_map(
        on_device, mesh=split, in_specs=in_specs, out_specs=out_specs, check_vma=False
    )
```

profile of v0, /device:TPU:1, one launch (start us, length us, event | category | flops | bytes accessed | tf_op | source)
XLA Modules:
  0.0 189.7 jit_solution(8125592697090335394)
XLA Ops:
  7.2 0.0 copy-start
  7.2 0.0 all-reduce.2.cloned.1.call-start
  7.2 1.2 copy-done
  8.4 1.3 fusion.3
  9.7 0.0 copy-start.2
  9.7 0.0 copy-start.3
  9.7 14.5 %psum.28 = f32[4,192,8]{1,2,0:T(8,128)S(1)} all-reduce(f32[4,192,8]{1,2,0:T(8,128)S(1)} %fusion.3), channel_id=1, replica_groups=mesh['dp_0'=4,'dp_1'=2,'tp'=16] {'dp_0'}, use_global_device_ids=true, to_apply=%region_0.0 | all-reduce | flops 6144 | bytes 49152 | tf_op jit(solution)/shard_map/psum | solution.py:14
  24.3 6.4 %psum.29 = f32[4,192,8]{1,2,0:T(8,128)S(1)} all-reduce(f32[4,192,8]{1,2,0:T(8,128)S(1)} %psum.28), channel_id=1, replica_groups=mesh['dp_0'=4,'dp_1'=2,'tp'=16] {'dp_1'}, use_global_device_ids=true, to_apply=%region_1.0 | all-reduce | flops 6144 | bytes 49152 | tf_op jit(solution)/shard_map/psum | solution.py:14
  30.6 0.9 fusion.5
  31.5 0.0 all-reduce.2.cloned.1.call-update
  31.6 0.2 convolution_multiply_fusion.1
  31.8 0.1 copy.13
  31.8 71.2 %psum.30 = f32[4,8,8]{1,2,0:T(8,128)S(1)} all-reduce(f32[4,8,8]{1,2,0:T(8,128)S(1)} %convolution_multiply_fusion.1), channel_id=1, replica_groups=mesh['dp_0'=4,'dp_1'=2,'tp'=16] {'dp_0','dp_1','tp'}, use_global_device_ids=true, to_apply=%region_2.0 | all-reduce | flops 256 | bytes 2048 | tf_op jit(solution)/shard_map/psum | solution.py:33
  103.0 0.1 copy.12
  103.2 0.6 gather_fusion
  103.8 0.1 multiply_add_fusion
  103.8 0.1 copy.14
  103.9 0.1 fusion.13
  104.0 2.9 %custom-call.9 = f32[4,8,8]{2,1,0:T(8,128)S(1)} custom-call(f32[4,8,8]{2,1,0:T(8,128)S(1)} %fusion.13), custom_call_target="Cholesky" | custom-call | tf_op jit(solution)/shard_map/jit(cholesky)/cholesky | solution.py:39
  106.9 0.1 select_reduce_fusion
  106.9 0.1 compare_reduce_fusion
  107.1 0.1 select_bitcast_fusion
  107.1 2.5 %custom-call.10 = f32[4,1,8,8]{2,3,1,0:T(8,128)S(1)} custom-call(f32[4,1,8,8]{3,2,1,0:T(8,128)S(1)} %select_bitcast_fusion), custom_call_target="InvertDiagBlocksLowerTriangular" | custom-call | tf_op jit(solution)/shard_map/triangular_solve | solution.py:43
  109.7 68.5 %all-reduce.2.cloned.1.call-done = f32[4,768,8]{1,2,0:T(8,128)} async-done(((f32[4,768,8]{1,2,0:T(8,128)}), f32[4,768,8]{1,2,0:T(8,128)}) %all-reduce.2.cloned.1.call-update) | async-done | bytes 98320 | tf_op jit(solution)/shard_map/psum | solution.py:33
  178.2 1.1 multiply_reduce_fusion
  179.2 1.0 fusion.11
  180.3 0.2 fusion.9
  180.4 0.0 copy-done.2
  180.4 0.0 copy-done.3
  180.4 1.7 multiply_subtract_fusion
  182.1 0.0 copy-done.1
  182.1 0.7 broadcast_multiply_fusion
  (8 shorter events, 0.1 us)
Async XLA Ops:
  7.2 1.3 copy-start
  7.2 171.0 %all-reduce.2.cloned.1.call-start = ((), (), s32[]{:S(2)}) async-start(), calls=%async_computation | async-start | bytes 196608 | tf_op jit(solution)/shard_map/psum | solution.py:33
  9.7 170.7 %copy-start.2 = (f32[4,192,96]{2,1,0:T(8,128)S(1)}, f32[4,192,96]{2,1,0:T(8,128)}, u32[]{:S(2)}) copy-start(f32[4,192,96]{2,1,0:T(8,128)} %param.6) | copy-start | bytes 884740
  9.7 170.7 %copy-start.3 = (f32[4,192,96]{2,1,0:T(8,128)S(1)}, f32[4,192,96]{2,1,0:T(8,128)}, u32[]{:S(2)}) copy-start(f32[4,192,96]{2,1,0:T(8,128)} %param.7) | copy-start | bytes 884740
  178.2 4.0 %copy-start.1 = (f32[4,768,8]{1,2,0:T(8,128)S(1)}, f32[4,768,8]{1,2,0:T(8,128)}, u32[]{:S(2)}) copy-start(f32[4,768,8]{1,2,0:T(8,128)} %all-reduce.2.cloned.1.call-done) | copy-start | bytes 294916
Sparse Core Ops, SparseCore 0:
  31.7 146.4 all-reduce.1
where the time goes:
time: 190 us
  blocking collectives  92.1 us (48%)
  waiting for transfers between devices  68.5 us (36%)
  between operations  14.1 us (7%)
  other arithmetic  7.66 us (4%)
  matrix products  5.23 us (3%)
  local copies, waits for them, and re-layouts  2.08 us (1%)
    psum x1, blocking collectives, on_device(): right, gram = lax.psum((part_right, own_share), DP_TP)  71.2 us
    psum x1, waiting for transfers between devices, on_device(): right, gram = lax.psum((part_right, own_share), DP_TP)  68.5 us
    psum x2, blocking collectives, by_axis(): x = lax.psum(x, axis)  20.9 us
  transfers between devices with their start and end apart: 1, of which 1 were waited for; matrix products, arithmetic and copies ran while one was open for 4% of the time, Pallas kernels for 0%

commit v1 on v0

--- a/solution.py
+++ b/solution.py
@@ -11,7 +11,8 @@
 
 def by_axis(x, axes):
     for axis in axes:
-        x = lax.psum(x, axis)
+        parts = lax.all_gather(x, axis, axis=0, tiled=False)
+        x = parts.sum(axis=0)
     return x
 
 

time: 190 us -> 183 us (0.963)
  blocking collectives: 92.1 us -> 84.2 us
    psum x2 -> x0, blocking collectives: 20.9 us -> none  [by_axis(): x = lax.psum(x, axis)]
    all_gather x0 -> x2, blocking collectives: none -> 14.1 us  [by_axis(): parts = lax.all_gather(x, axis, axis=0, tiled=False)]
where the time goes in v1:
time: 183 us
  blocking collectives  84.2 us (46%)
  waiting for transfers between devices  69.2 us (38%)
  between operations  14.1 us (8%)
  other arithmetic  7.68 us (4%)
  matrix products  5.22 us (3%)
  local copies, waits for them, and re-layouts  2.08 us (1%)
    psum x1, blocking collectives, on_device(): right, gram = lax.psum((part_right, own_share), DP_TP)  70.1 us
    psum x1, waiting for transfers between devices, on_device(): right, gram = lax.psum((part_right, own_share), DP_TP)  69.2 us
    all_gather x2, blocking collectives, by_axis(): parts = lax.all_gather(x, axis, axis=0, tiled=False)  14.1 us
  transfers between devices with their start and end apart: 1, of which 1 were waited for; matrix products, arithmetic and copies ran while one was open for 4% of the time, Pallas kernels for 0%

profile of v1, /device:TPU:1, one launch (start us, length us, event | category | flops | bytes accessed | tf_op | source)
XLA Modules:
  0.0 182.5 jit_solution(17034316184257275074)
XLA Ops:
  7.2 0.0 copy-start
  7.2 0.0 all-reduce.2.cloned.1.call-start
  7.2 1.2 copy-done
  8.4 1.3 fusion.3
  9.7 10.6 %all-gather = f32[16,192,8]{1,2,0:T(8,128)S(1)} all-gather(f32[4,192,8]{1,2,0:T(8,128)S(1)} %fusion.3), channel_id=2, replica_groups=mesh['dp_0'=4,'dp_1'=2,'tp'=16] {'dp_0'}, dimensions={0}, use_global_device_ids=true | all-gather | bytes 122880 | tf_op jit(solution)/shard_map/all_gather | solution.py:14
  20.3 0.0 copy-start.2
  20.3 0.0 copy-start.3
  20.3 3.6 %all-gather.1 = f32[8,192,8]{1,2,0:T(8,128)S(1)} all-gather(f32[4,192,8]{1,2,0:T(8,128)S(1)} %reduce_sum.36), channel_id=3, replica_groups=mesh['dp_0'=4,'dp_1'=2,'tp'=16] {'dp_1'}, dimensions={0}, use_global_device_ids=true | all-gather | bytes 73728 | tf_op jit(solution)/shard_map/all_gather | solution.py:14
  23.9 0.9 fusion.5
  24.8 0.0 all-reduce.2.cloned.1.call-update
  24.9 0.2 convolution_multiply_fusion.1
  25.0 0.1 copy.17
  25.1 70.1 %psum.14 = f32[4,8,8]{1,2,0:T(8,128)S(1)} all-reduce(f32[4,8,8]{1,2,0:T(8,128)S(1)} %convolution_multiply_fusion.1), channel_id=1, replica_groups=mesh['dp_0'=4,'dp_1'=2,'tp'=16] {'dp_0','dp_1','tp'}, use_global_device_ids=true, to_apply=%region_2.0 | all-reduce | flops 256 | bytes 2048 | tf_op jit(solution)/shard_map/psum | solution.py:34
  95.2 0.1 copy.16
  95.3 0.6 gather_fusion
  95.9 0.1 multiply_add_fusion
  96.0 0.1 copy.18
  96.1 0.1 fusion.13
  96.1 2.9 %custom-call.9 = f32[4,8,8]{2,1,0:T(8,128)S(1)} custom-call(f32[4,8,8]{2,1,0:T(8,128)S(1)} %fusion.13), custom_call_target="Cholesky" | custom-call | tf_op jit(solution)/shard_map/jit(cholesky)/cholesky | solution.py:40
  99.0 0.1 select_reduce_fusion
  99.1 0.1 compare_reduce_fusion
  99.2 0.1 select_bitcast_fusion
  99.3 2.5 %custom-call.10 = f32[4,1,8,8]{2,3,1,0:T(8,128)S(1)} custom-call(f32[4,1,8,8]{3,2,1,0:T(8,128)S(1)} %select_bitcast_fusion), custom_call_target="InvertDiagBlocksLowerTriangular" | custom-call | tf_op jit(solution)/shard_map/triangular_solve | solution.py:44
  101.8 69.2 %all-reduce.2.cloned.1.call-done = f32[4,768,8]{1,2,0:T(8,128)} async-done(((f32[4,768,8]{1,2,0:T(8,128)}), f32[4,768,8]{1,2,0:T(8,128)}) %all-reduce.2.cloned.1.call-update) | async-done | bytes 98320 | tf_op jit(solution)/shard_map/psum | solution.py:34
  171.0 1.1 multiply_reduce_fusion
  172.1 1.0 fusion.11
  173.1 0.2 fusion.9
  173.2 0.0 copy-done.2
  173.2 0.0 copy-done.3
  173.3 1.7 multiply_subtract_fusion
  175.0 0.0 copy-done.1
  175.0 0.7 broadcast_multiply_fusion
  (10 shorter events, 0.1 us)
Async XLA Ops:
  7.2 1.3 copy-start
  7.2 163.8 %all-reduce.2.cloned.1.call-start = ((), (), s32[]{:S(2)}) async-start(), calls=%async_computation | async-start | bytes 196608 | tf_op jit(solution)/shard_map/psum | solution.py:34
  20.3 153.0 %copy-start.2 = (f32[4,192,96]{2,1,0:T(8,128)S(1)}, f32[4,192,96]{2,1,0:T(8,128)}, u32[]{:S(2)}) copy-start(f32[4,192,96]{2,1,0:T(8,128)} %param.6) | copy-start | bytes 884740
  20.3 153.0 %copy-start.3 = (f32[4,192,96]{2,1,0:T(8,128)S(1)}, f32[4,192,96]{2,1,0:T(8,128)}, u32[]{:S(2)}) copy-start(f32[4,192,96]{2,1,0:T(8,128)} %param.7) | copy-start | bytes 884740
  171.0 4.0 %copy-start.1 = (f32[4,768,8]{1,2,0:T(8,128)S(1)}, f32[4,768,8]{1,2,0:T(8,128)}, u32[]{:S(2)}) copy-start(f32[4,768,8]{1,2,0:T(8,128)} %all-reduce.2.cloned.1.call-done) | copy-start | bytes 294916
Sparse Core Ops, SparseCore 0:
  24.9 145.9 all-reduce.1
